TPU v7x, 256 devices: a whole 4x4x8 slice. The times are simulated.
256 devices in a mesh: row: 16 (over y, x), col: 16 (over z, core).
Axes of the slice: x: 4, y: 4, z: 8, core: 2. Of those that a mesh axis runs over, the one named last changes fastest.
Arguments:
- tokens: bfloat16 [1024, 7168], P('col', 'row'), may hold values from -6 to 6
- routes: int32 [1024, 8], P('col'), may hold values from 0 to 31, all different within a row; in each aligned block of 64 rows (0 to 63, 64 to 127, ...) at most 40 rows name the same one
- gates: float32 [1024, 8], P('col'), may hold values from 0.05 to 0.5
- w_gate: bfloat16 [32, 7168, 2048], P('col', None, 'row'), may hold values from -0.0625 to 0.0625
- w_up: bfloat16 [32, 7168, 2048], P('col', None, 'row'), may hold values from -0.0625 to 0.0625
- w_down: bfloat16 [32, 2048, 7168], P('col', 'row'), may hold values from -0.125 to 0.125
Outputs:
- mixed: bfloat16 [1024, 7168], P('col', 'row')
Inputs may be any that keep to these rules, and one draw needn't show every extreme that they name: `routes`: the 8 experts of a token are distinct. Among the 64 tokens of one index of col (aligned blocks of 64 tokens), no expert is chosen more than 40 times, and some expert is chosen exactly 40 times.
All inputs are finite; a program needn't handle non-finite values.
Results may differ from a plain program's by a relative error of at most 0.015.
Values may be sent and summed in bfloat16 or wider, within the bound.
No kernel may reach another device: no remote copies, remote signals or barrier semaphores. Data moves between devices by JAX's collectives and lax.ppermute only.
A program may use at most 128 MiB of HBM per device.

v0:
```python
import jax
import jax.numpy as jnp
from jax import lax
from jax.sharding import PartitionSpec as P

CAP = 40


def group_positions(grouped, expert_count):
    onehot = (
        grouped[:, :, None] == jnp.arange(expert_count, dtype=jnp.int32)[None, None, :]
    ).astype(jnp.int32)
    before = jnp.cumsum(onehot, axis=1) - onehot
    return jnp.sum(before * onehot, axis=2)


def shards(tokens, routes, gates, w_gate, w_up, w_down):
    held_experts = w_gate.shape[0]
    unit_count = w_gate.shape[2]
    group_count = lax.axis_size("col")
    expert_count = held_experts * group_count
    tok_rows, top_count = routes.shape
    slot_count = CAP * group_count
    flat_routes = routes.reshape(1, tok_rows * top_count)
    position = group_positions(flat_routes, expert_count)[0]
    target = flat_routes[0] * CAP + position
    owner_rows = jnp.arange(tok_rows * top_count, dtype=jnp.int32) // top_count
    outgoing = jnp.zeros((expert_count * CAP, tokens.shape[1]), jnp.bfloat16)
    outgoing = (
        outgoing.at[target].set(tokens[owner_rows]).reshape(expert_count, CAP, tokens.shape[1])
    )
    arrived = lax.all_to_all(outgoing, "col", split_axis=0, concat_axis=1, tiled=True)
    piece = lax.all_gather(arrived, "row", axis=2, tiled=True)
    gate_act = jnp.einsum("erd,edf->erf", piece, w_gate, preferred_element_type=jnp.float32)
    up_act = jnp.einsum("erd,edf->erf", piece, w_up, preferred_element_type=jnp.float32)
    hidden = (jax.nn.silu(gate_act) * up_act).astype(jnp.bfloat16)
    columns = lax.all_to_all(w_down, "row", split_axis=2, concat_axis=1, tiled=True)
    wide_hidden = lax.all_gather(hidden, "row", axis=2, tiled=True)
    blocks = lax.axis_size("row")
    partial_value = jnp.einsum(
        "ercf,ecfd->ecrd",
        wide_hidden.reshape(held_experts, slot_count, blocks, unit_count),
        columns.reshape(held_experts, blocks, unit_count, columns.shape[2]),
        preferred_element_type=jnp.float32,
    )
    rounded = lax.optimization_barrier(partial_value.astype(jnp.bfloat16))
    result = jnp.sum(rounded.astype(jnp.float32), axis=1).astype(jnp.bfloat16)
    returned = lax.all_to_all(result, "col", split_axis=1, concat_axis=0, tiled=True)
    picked = returned.reshape(expert_count * CAP, returned.shape[2])[target]
    picked = picked.reshape(tok_rows, top_count, returned.shape[2])
    mixed = jnp.sum(gates[:, :, None] * picked.astype(jnp.float32), axis=1)
    return mixed.astype(jnp.bfloat16)


def solution(mesh):
    return jax.shard_map(
        shards,
        mesh=mesh,
        in_specs=(
            P("col", "row"),
            P("col", None),
            P("col", None),
            P("col", None, "row"),
            P("col", None, "row"),
            P("col", "row", None),
        ),
        out_specs=P("col", "row"),
        check_vma=False,
    )
```

profile of v0, /device:TPU:1, one launch (start us, length us, event | category | flops | bytes accessed | tf_op | source)
XLA Modules:
  0.0 376.0 jit_solution(8991820587349833042)
XLA Ops:
  6.5 0.0 copy-start
  6.5 0.0 all-gather.3.cloned.1.call-start
  6.5 0.8 copy.23
  7.3 0.1 eq.27
  7.4 0.1 compare_convert_fusion
  7.5 1.2 reduce-window.6
  8.7 0.2 slice_reduce_fusion
  8.9 0.1 copy.25
  9.0 0.7 broadcast_multiply_fusion
  9.7 0.1 copy.26
  9.8 0.1 copy.22
  9.9 0.1 mul.37
  10.0 0.1 broadcast.138
  10.1 0.1 fusion.7
  10.2 0.0 copy-done
  10.2 5.2 %scatter_custom_fusion = bf16[1280,448]{1,0:T(8,128)(2,1)S(1)} fusion(s32[512]{0:T(512)S(1)} %bitcast.54, bf16[]{:T(256)} %constant.27.clone.1, bf16[64,448]{1,0:T(8,128)(2,1)S(1)} %copy-done, s32[1024]{0:T(1024)S(1)} %pad_clamp_fusion.1), kind=kCustom, calls=%fused_computation.10 | custom fusion | bytes 1146882 | tf_op jit(solution)/shard_map/scatter | solution.py:30
  15.4 43.8 %all_to_all.48 = bf16[32,40,448]{2,1,0:T(8,128)(2,1)S(1)} all-to-all(bf16[32,40,448]{2,1,0:T(8,128)(2,1)S(1)} %bitcast.46), channel_id=1, replica_groups=mesh['row'=16,'col'=16] {'col'}, dimensions={0} | all-to-all | bytes 2293760 | tf_op jit(solution)/shard_map/all_to_all | solution.py:32
  59.2 0.1 copy.27
  59.3 1.4 copy.28
  60.8 0.0 all-gather.3.cloned.1.call-update
  60.8 0.2 all-gather.5.cloned.1.call-start
  61.0 120.8 %all-gather.3.cloned.1.call-done = bf16[2,640,7168]{1,2,0:T(8,128)(2,1)} async-done(((bf16[2,640,448]{1,2,0:T(8,128)(2,1)}), bf16[2,640,7168]{1,2,0:T(8,128)(2,1)}) %all-gather.3.cloned.1.call-update) | async-done | bytes 18350096 | tf_op jit(solution)/shard_map/all_gather | solution.py:33
  181.8 0.0 copy-start.2
  181.8 11.6 %fusion.8 = f32[2,640,128]{2,1,0:T(8,128)S(1)} fusion(bf16[2,640,7168]{1,2,0:T(8,128)(2,1)} %all-gather.3.cloned.1.call-done, bf16[2,7168,128]{2,1,0:T(8,128)(2,1)} %param.9), kind=kOutput, calls=%fused_computation.28 | convolution fusion | flops 2348810240 | bytes 22675456 | tf_op jit(solution)/shard_map/erd,edf->erf/dot_general | solution.py:34
  193.4 0.0 copy-done.2
  193.5 11.9 %fusion.2 = bf16[2,640,128]{2,1,0:T(8,128)(2,1)} fusion(bf16[2,640,7168]{1,2,0:T(8,128)(2,1)} %all-gather.3.cloned.1.call-done, bf16[2,7168,128]{2,1,0:T(8,128)(2,1)S(1)} %copy-done.2, f32[2,640,128]{2,1,0:T(8,128)S(1)} %fusion.8), kind=kOutput, calls=%fused_computation.7 | convolution fusion | flops 2349793280 | bytes 23003136 | tf_op jit(solution)/shard_map/erd,edf->erf/dot_general | solution.py:35
  205.3 0.0 all-gather.5.cloned.1.call-update
  205.3 9.9 %copy.29 = bf16[2,128,7168]{1,0,2:T(2,128)(2,1)} copy(bf16[2,128,7168]{2,1,0:T(8,128)(2,1)} %param.11) | data formatting | bytes 7340032 | tf_op args[5]
  215.2 52.8 %all_to_all.49 = bf16[2,128,7168]{1,0,2:T(2,128)(2,1)S(1)} all-to-all(bf16[2,128,7168]{1,0,2:T(2,128)(2,1)} %copy.29), channel_id=1, replica_groups=mesh['row'=16,'col'=16] {'row'}, dimensions={2} | all-to-all | bytes 7340032 | tf_op jit(solution)/shard_map/all_to_all | solution.py:37
  268.0 2.4 copy.30
  270.4 28.9 %all-gather.5.cloned.1.call-done = bf16[2,640,2048]{2,1,0:T(8,128)(2,1)} async-done(((bf16[2,640,128]{2,1,0:T(8,128)(2,1)}), bf16[2,640,2048]{2,1,0:T(8,128)(2,1)}) %all-gather.5.cloned.1.call-update) | async-done | bytes 5242896 | tf_op jit(solution)/shard_map/all_gather | solution.py:38
  299.2 12.0 %convolution_convert_fusion = bf16[2,16,640,448]{2,3,1,0:T(8,128)(2,1)} fusion(bf16[2,16,128,448]{2,3,1,0:T(8,128)(2,1)} %bitcast.44, bf16[2,640,2048]{2,1,0:T(8,128)(2,1)} %all-gather.5.cloned.1.call-done), kind=kOutput, calls=%fused_computation.3 | convolution fusion | flops 2357985280 | bytes 27262976 | tf_op jit(solution)/shard_map/ercf,ecfd->ecrd/dot_general | solution.py:40
  311.2 9.4 %reduce_sum.34 = bf16[2,640,448]{1,2,0:T(8,128)(2,1)S(1)} reduce(bf16[2,16,640,448]{2,3,1,0:T(8,128)(2,1)} %convolution_convert_fusion, bf16[]{:T(256)} %constant.27.clone.1), dimensions={1}, to_apply=%region_4.5 | reduce | flops 8601600 | bytes 19496962 | tf_op jit(solution)/shard_map/reduce_sum | solution.py:47
  320.7 0.0 copy-start.3
  320.7 2.8 copy.32
  323.5 9.1 %all-to-all-start.2 = ((bf16[2,640,448]{2,0,1:T(2,128)(2,1)}), bf16[2,640,448]{2,0,1:T(2,128)(2,1)S(1)}, u32[]{:S(2)}, u32[]{:S(2)}) async-start(bf16[2,640,448]{2,0,1:T(2,128)(2,1)} %copy.32), calls=%async_computation.2 | async-start | bytes 2621440 | tf_op jit(solution)/shard_map/all_to_all | solution.py:48
  332.5 0.0 copy-done.3
  332.5 0.1 copy.21
  332.6 33.2 %all-to-all-done.2 = bf16[2,640,448]{2,0,1:T(2,128)(2,1)S(1)} async-done(((bf16[2,640,448]{2,0,1:T(2,128)(2,1)}), bf16[2,640,448]{2,0,1:T(2,128)(2,1)S(1)}, u32[]{:S(2)}, u32[]{:S(2)}) %all-to-all-start.2) | async-done | bytes 1146912 | tf_op jit(solution)/shard_map/all_to_all | solution.py:48
  365.8 0.2 copy.33
  366.0 0.0 copy-start.1
  366.0 0.1 copy.34
  366.1 2.0 gather_fusion
  368.1 1.0 fusion.3
  369.1 0.0 copy-done.1
  (7 shorter events, 0.1 us)
Async XLA Ops:
  6.5 3.7 copy-start
  6.5 175.3 %all-gather.3.cloned.1.call-start = ((), (), s32[]{:S(2)}) async-start(), calls=%async_computation.3 | async-start | bytes 19496960 | tf_op jit(solution)/shard_map/all_gather | solution.py:33
  60.8 238.5 %all-gather.5.cloned.1.call-start = ((), (), s32[]{:S(2)}) async-start(), calls=%async_computation.4 | async-start | bytes 5570560 | tf_op jit(solution)/shard_map/all_gather | solution.py:38
  181.8 11.6 %copy-start.2 = (bf16[2,7168,128]{2,1,0:T(8,128)(2,1)S(1)}, bf16[2,7168,128]{2,1,0:T(8,128)(2,1)}, u32[]{:S(2)}) copy-start(bf16[2,7168,128]{2,1,0:T(8,128)(2,1)} %param.10) | copy-start | bytes 11010052
  320.7 11.9 %copy-start.3 = (f32[64,8]{0,1:T(8,128)S(1)}, f32[64,8]{0,1:T(8,128)}, u32[]{:S(2)}) copy-start(f32[64,8]{0,1:T(8,128)} %param.8) | copy-start | bytes 6148
  323.5 42.3 %all-to-all-start.2 = ((bf16[2,640,448]{2,0,1:T(2,128)(2,1)}), bf16[2,640,448]{2,0,1:T(2,128)(2,1)S(1)}, u32[]{:S(2)}, u32[]{:S(2)}) async-start(bf16[2,640,448]{2,0,1:T(2,128)(2,1)} %copy.32), calls=%async_computation.2 | async-start | bytes 2621440 | tf_op jit(solution)/shard_map/all_to_all | solution.py:48
  366.0 3.2 copy-start.1
Sparse Core Ops, SparseCore 0:
  60.9 120.8 all-gather.2
  205.5 93.7 all-gather.4
where the time goes:
time: 377 us; the launch traced here: 376 us
  waiting for transfers between devices  183 us (49%)
  blocking collectives  96.6 us (26%)
  matrix products  35.5 us (9%)
  local copies, waits for them, and re-layouts  25.7 us (7%)
  between operations  13.5 us (4%)
  other arithmetic  12.6 us (3%)
  starting transfers between devices  9.29 us (2%)
    all_gather x1, waiting for transfers between devices, shards(): piece = lax.all_gather(arrived, 'row', axis=2, tiled=True)  121 us
    all_to_all x1, blocking collectives, shards(): lax.all_to_all(w_down, 'row', split_axis=2, concat_axis=1, tiled=True)  52.8 us
    all_to_all x1, blocking collectives, shards(): lax.all_to_all(outgoing, 'col', split_axis=0, concat_axis=1, tiled=True)  43.8 us
    all_to_all x1, waiting for transfers between devices, shards(): lax.all_to_all(result, 'col', split_axis=1, concat_axis=0, tiled=True)  33.2 us
    all_gather x1, waiting for transfers between devices, shards(): wide_hidden = lax.all_gather(hidden, 'row', axis=2, tiled=True)  28.9 us
    dot_general x1, matrix products, shards(): jnp.einsum('ercf,ecfd->ecrd', wide_hidden.reshape(held_experts, slot_coun...  12 us
    dot_general x1, matrix products, shards(): jnp.einsum('erd,edf->erf', piece, w_up, preferred_element_type=jnp.float32)  11.9 us
    dot_general x1, matrix products, shards(): jnp.einsum('erd,edf->erf', piece, w_gate, preferred_element_type=jnp.floa...  11.6 us
  transfers between devices with their start and end apart: 3, of which 3 were waited for; matrix products, arithmetic and copies ran while one was open for 3% of the time, Pallas kernels for 0%

commit v1 on v0

--- a/solution.py
+++ b/solution.py
@@ -4,6 +4,11 @@
 from jax.sharding import PartitionSpec as P
 
 CAP = 40
+
+
+def swapped_in(array, axis, dim):
+    outgoing = jnp.stack([array] * lax.axis_size(axis))
+    return jnp.concatenate(lax.all_to_all(outgoing, axis, 0, 0), axis=dim)
 
 
 def group_positions(grouped, expert_count):
@@ -30,7 +35,7 @@
         outgoing.at[target].set(tokens[owner_rows]).reshape(expert_count, CAP, tokens.shape[1])
     )
     arrived = lax.all_to_all(outgoing, "col", split_axis=0, concat_axis=1, tiled=True)
-    piece = lax.all_gather(arrived, "row", axis=2, tiled=True)
+    piece = swapped_in(arrived, "row", 2)
     gate_act = jnp.einsum("erd,edf->erf", piece, w_gate, preferred_element_type=jnp.float32)
     up_act = jnp.einsum("erd,edf->erf", piece, w_up, preferred_element_type=jnp.float32)
     hidden = (jax.nn.silu(gate_act) * up_act).astype(jnp.bfloat16)

time: 377 us -> 474 us (1.26)
  blocking collectives: 96.6 us -> 306 us
  waiting for transfers between devices: 183 us -> 63.3 us
  local copies, waits for them, and re-layouts: 25.7 us -> 34.2 us
    all_to_all x0 -> x1, blocking collectives: none -> 210 us  [swapped_in(): return jnp.concatenate(lax.all_to_all(outgoing, axis, 0, 0), axis=dim)]
    all_gather x1 -> x0, waiting for transfers between devices: 121 us -> none  [shards(): piece = lax.all_gather(arrived, 'row', axis=2, tiled=True)]
    all_to_all x0 -> x1, local copies, waits for them, and re-layouts: none -> 6.95 us  [swapped_in(): return jnp.concatenate(lax.all_to_all(outgoing, axis, 0, 0), axis=dim)]
    unnamed x11 -> x13, local copies, waits for them, and re-layouts: 10.8 us -> 10.8 us
  transfers between devices with their start and end apart: 3 -> 2, of which waited for: 3 -> 2; matrix products, arithmetic and copies ran while one was open for 3% -> 3% of each run, Pallas kernels for 0% -> 0%
where the time goes in v1:
time: 474 us; the launch traced here: 473 us
  blocking collectives  306 us (65%)
  waiting for transfers between devices  63.3 us (13%)
  matrix products  35 us (7%)
  local copies, waits for them, and re-layouts  34.2 us (7%)
  between operations  13.5 us (3%)
  other arithmetic  12.6 us (3%)
  starting transfers between devices  9.06 us (2%)
    all_to_all x1, blocking collectives, swapped_in(): return jnp.concatenate(lax.all_to_all(outgoing, axis, 0, 0), axis=dim)  210 us
    all_to_all x1, blocking collectives, shards(): lax.all_to_all(w_down, 'row', split_axis=2, concat_axis=1, tiled=True)  51.3 us
    all_to_all x1, blocking collectives, shards(): lax.all_to_all(outgoing, 'col', split_axis=0, concat_axis=1, tiled=True)  43.8 us
    all_to_all x1, waiting for transfers between devices, shards(): lax.all_to_all(result, 'col', split_axis=1, concat_axis=0, tiled=True)  33.2 us
    all_gather x1, waiting for transfers between devices, shards(): wide_hidden = lax.all_gather(hidden, 'row', axis=2, tiled=True)  30.1 us
    dot_general x1, matrix products, shards(): jnp.einsum('ercf,ecfd->ecrd', wide_hidden.reshape(held_experts, slot_coun...  12 us
    dot_general x1, matrix products, shards(): jnp.einsum('erd,edf->erf', piece, w_up, preferred_element_type=jnp.float32)  11.9 us
    dot_general x1, matrix products, shards(): jnp.einsum('erd,edf->erf', piece, w_gate, preferred_element_type=jnp.floa...  11.2 us
  transfers between devices with their start and end apart: 2, of which 2 were waited for; matrix products, arithmetic and copies ran while one was open for 3% of the time, Pallas kernels for 0%

profile of v1, /device:TPU:1, one launch (start us, length us, event | category | flops | bytes accessed | tf_op | source)
XLA Modules:
  0.0 473.2 jit_solution(10824859618947674513)
XLA Ops:
  6.5 0.0 copy-start
  6.5 0.0 all-gather.2.cloned.1.call-start
  6.5 0.8 copy.36
  7.3 0.1 eq.27
  7.4 0.1 compare_convert_fusion
  7.5 1.2 reduce-window.6
  8.7 0.2 slice_reduce_fusion
  8.9 0.1 copy.38
  9.0 0.7 broadcast_multiply_fusion
  9.7 0.1 copy.39
  9.8 0.1 copy.35
  9.9 0.1 mul.37
  10.0 0.1 broadcast.139
  10.1 0.1 fusion.7
  10.2 0.0 copy-done
  10.2 5.2 %scatter_custom_fusion = bf16[1280,448]{1,0:T(8,128)(2,1)S(1)} fusion(s32[512]{0:T(512)S(1)} %bitcast.59, bf16[]{:T(256)} %constant.27.clone.1, bf16[64,448]{1,0:T(8,128)(2,1)S(1)} %copy-done, s32[1024]{0:T(1024)S(1)} %pad_clamp_fusion.1), kind=kCustom, calls=%fused_computation.10 | custom fusion | bytes 1146882 | tf_op jit(solution)/shard_map/scatter | solution.py:35
  15.4 43.8 %all_to_all.50 = bf16[32,40,448]{2,1,0:T(8,128)(2,1)S(1)} all-to-all(bf16[32,40,448]{2,1,0:T(8,128)(2,1)S(1)} %bitcast.51), channel_id=1, replica_groups=mesh['row'=16,'col'=16] {'col'}, dimensions={0} | all-to-all | bytes 2293760 | tf_op jit(solution)/shard_map/all_to_all | solution.py:37
  59.2 0.1 copy.40
  59.3 0.7 copy.41
  60.1 2.3 stack.5
  62.3 210.5 %all_to_all.51 = bf16[16,2,640,448]{2,3,1,0:T(8,128)(2,1)S(1)} all-to-all(bf16[16,2,640,448]{2,3,1,0:T(8,128)(2,1)S(1)} %stack.5), channel_id=1, replica_groups=mesh['row'=16,'col'=16] {'row'}, dimensions={0} | all-to-all | bytes 36700160 | tf_op jit(solution)/shard_map/all_to_all | solution.py:11
  272.8 0.0 copy-start.2
  272.8 6.9 %copy.42 = bf16[16,2,640,448]{2,3,0,1:T(8,128)(2,1)} copy(bf16[16,2,640,448]{2,3,1,0:T(8,128)(2,1)S(1)} %all_to_all.51) | data formatting | bytes 36700160 | tf_op jit(solution)/shard_map/all_to_all | solution.py:11
  279.8 0.0 copy-done.2
  279.8 0.0 copy-start.3
  279.8 11.2 %fusion.8 = f32[2,640,128]{2,1,0:T(8,128)S(1)} fusion(bf16[2,640,7168]{1,2,0:T(8,128)(2,1)} %bitcast.47, bf16[2,7168,128]{2,1,0:T(8,128)(2,1)S(1)} %copy-done.2), kind=kOutput, calls=%fused_computation.28 | convolution fusion | flops 2348810240 | bytes 22675456 | tf_op jit(solution)/shard_map/erd,edf->erf/dot_general | solution.py:39
  291.0 0.0 copy-done.3
  291.0 11.9 %fusion.2 = bf16[2,640,128]{2,1,0:T(8,128)(2,1)} fusion(bf16[2,640,7168]{1,2,0:T(8,128)(2,1)} %bitcast.48, bf16[2,7168,128]{2,1,0:T(8,128)(2,1)S(1)} %copy-done.3, f32[2,640,128]{2,1,0:T(8,128)S(1)} %fusion.8), kind=kOutput, calls=%fused_computation.7 | convolution fusion | flops 2349793280 | bytes 23003136 | tf_op jit(solution)/shard_map/erd,edf->erf/dot_general | solution.py:40
  302.8 0.0 all-gather.2.cloned.1.call-update
  302.9 9.9 %copy.45 = bf16[2,128,7168]{1,0,2:T(2,128)(2,1)} copy(bf16[2,128,7168]{2,1,0:T(8,128)(2,1)} %param.11) | data formatting | bytes 7340032 | tf_op args[5]
  312.8 51.3 %all_to_all.52 = bf16[2,128,7168]{1,0,2:T(2,128)(2,1)S(1)} all-to-all(bf16[2,128,7168]{1,0,2:T(2,128)(2,1)} %copy.45), channel_id=1, replica_groups=mesh['row'=16,'col'=16] {'row'}, dimensions={2} | all-to-all | bytes 7340032 | tf_op jit(solution)/shard_map/all_to_all | solution.py:42
  364.1 2.4 copy.46
  366.4 30.1 %all-gather.2.cloned.1.call-done = bf16[2,640,2048]{2,1,0:T(8,128)(2,1)} async-done(((bf16[2,640,128]{2,1,0:T(8,128)(2,1)}), bf16[2,640,2048]{2,1,0:T(8,128)(2,1)}) %all-gather.2.cloned.1.call-update) | async-done | bytes 5242896 | tf_op jit(solution)/shard_map/all_gather | solution.py:43
  396.5 12.0 %convolution_convert_fusion = bf16[2,16,640,448]{2,3,1,0:T(8,128)(2,1)} fusion(bf16[2,16,128,448]{2,3,1,0:T(8,128)(2,1)} %bitcast.49, bf16[2,640,2048]{2,1,0:T(8,128)(2,1)} %all-gather.2.cloned.1.call-done), kind=kOutput, calls=%fused_computation.3 | convolution fusion | flops 2357985280 | bytes 27262976 | tf_op jit(solution)/shard_map/ercf,ecfd->ecrd/dot_general | solution.py:45
  408.5 9.4 %reduce_sum.34 = bf16[2,640,448]{1,2,0:T(8,128)(2,1)S(1)} reduce(bf16[2,16,640,448]{2,3,1,0:T(8,128)(2,1)} %convolution_convert_fusion, bf16[]{:T(256)} %constant.27.clone.1), dimensions={1}, to_apply=%region_4.5 | reduce | flops 8601600 | bytes 19496962 | tf_op jit(solution)/shard_map/reduce_sum | solution.py:52
  417.9 0.0 copy-start.4
  417.9 2.8 copy.48
  420.7 9.1 %all-to-all-start.3 = ((bf16[2,640,448]{2,0,1:T(2,128)(2,1)}), bf16[2,640,448]{2,0,1:T(2,128)(2,1)S(1)}, u32[]{:S(2)}, u32[]{:S(2)}) async-start(bf16[2,640,448]{2,0,1:T(2,128)(2,1)} %copy.48), calls=%async_computation.3 | async-start | bytes 2621440 | tf_op jit(solution)/shard_map/all_to_all | solution.py:53
  429.8 0.0 copy-done.4
  429.8 0.1 copy.34
  429.9 33.2 %all-to-all-done.3 = bf16[2,640,448]{2,0,1:T(2,128)(2,1)S(1)} async-done(((bf16[2,640,448]{2,0,1:T(2,128)(2,1)}), bf16[2,640,448]{2,0,1:T(2,128)(2,1)S(1)}, u32[]{:S(2)}, u32[]{:S(2)}) %all-to-all-start.3) | async-done | bytes 1146912 | tf_op jit(solution)/shard_map/all_to_all | solution.py:53
  463.0 0.2 copy.49
  463.2 0.0 copy-start.1
  463.3 0.1 copy.50
  463.4 2.0 gather_fusion
  465.4 1.0 fusion.3
  466.4 0.0 copy-done.1
  (7 shorter events, 0.1 us)
Async XLA Ops:
  6.5 3.7 copy-start
  6.5 390.0 %all-gather.2.cloned.1.call-start = ((), (), s32[]{:S(2)}) async-start(), calls=%async_computation.4 | async-start | bytes 5570560 | tf_op jit(solution)/shard_map/all_gather | solution.py:43
  272.8 7.0 %copy-start.2 = (bf16[2,7168,128]{2,1,0:T(8,128)(2,1)S(1)}, bf16[2,7168,128]{2,1,0:T(8,128)(2,1)}, u32[]{:S(2)}) copy-start(bf16[2,7168,128]{2,1,0:T(8,128)(2,1)} %param.9) | copy-start | bytes 11010052
  279.8 11.2 %copy-start.3 = (bf16[2,7168,128]{2,1,0:T(8,128)(2,1)S(1)}, bf16[2,7168,128]{2,1,0:T(8,128)(2,1)}, u32[]{:S(2)}) copy-start(bf16[2,7168,128]{2,1,0:T(8,128)(2,1)} %param.10) | copy-start | bytes 11010052
  417.9 11.8 %copy-start.4 = (f32[64,8]{0,1:T(8,128)S(1)}, f32[64,8]{0,1:T(8,128)}, u32[]{:S(2)}) copy-start(f32[64,8]{0,1:T(8,128)} %param.8) | copy-start | bytes 6148
  420.7 42.3 %all-to-all-start.3 = ((bf16[2,640,448]{2,0,1:T(2,128)(2,1)}), bf16[2,640,448]{2,0,1:T(2,128)(2,1)S(1)}, u32[]{:S(2)}, u32[]{:S(2)}) async-start(bf16[2,640,448]{2,0,1:T(2,128)(2,1)} %copy.48), calls=%async_computation.3 | async-start | bytes 2621440 | tf_op jit(solution)/shard_map/all_to_all | solution.py:53
  463.2 3.2 copy-start.1
Sparse Core Ops, SparseCore 0:
  303.0 93.4 all-gather.1
